TPU v7x, 32 devices: a whole 2x2x4 slice. The times are simulated.
32 devices in a mesh: field: 2 (over x), ep: 16 (over z, y, core).
Axes of the slice: x: 2, y: 2, z: 4, core: 2. Of those that a mesh axis runs over, the one named last changes fastest.
Arguments:
- images: float32 [64, 16, 256], P(('field', 'ep')), parts along dimension 0, may hold values from -6 to 6
- reference_image: float32 [32, 256], P('field'), parts along dimension 0, may hold values from -6 to 6
- kernels: float32 [16, 23, 23], replicated, may hold values from -0.25 to 0.25
- kernel_index: int32 [64], P(('field', 'ep')), parts along dimension 0, may hold values from 0 to 15
- tile_mask: int32 [64, 16, 2], P(('field', 'ep')), parts along dimension 0, may hold values 0 or 1
- systematics: float32 [64, 40], P('field'), parts along dimension 0, may hold values from -6 to 6
- onsets: int32 [16], P('field'), parts along dimension 0, may hold values from 0 to 27
Outputs:
- coefficients: float32 [48, 32, 256], P(None, ('field', 'ep')), parts along dimension 1
- epoch_scatter: float32 [64], P('field'), parts along dimension 0
There are 2 independent parts, one for each index of `field`. A program takes and returns all parts, laid end to end along the dimension named above; an argument that names none is the same for every part. Nothing has to cross between parts.
All inputs are finite; a program needn't handle non-finite values. No bound on the sum of `tile_mask` on one device may be relied on, other than what follows from the above.
Results may differ from a plain program's by a relative error of at most 0.00011.
Values sent between devices are 32-bit elements; how exact they have to be, the bound alone decides.
A program may use at most 64 MiB of HBM per device.

v0:
```python
import math
import jax
import jax.numpy as jnp
from jax import lax
from jax.sharding import PartitionSpec as P

cov_ridge = 0.5
fit_ridge = 1.0


def correlate(stack, chosen):
    count, rows, width = stack.shape
    side = chosen.shape[1]
    half = (side - 1) // 2
    padded = jnp.pad(stack, ((0, 0), (half, half), (half, half)))
    filters = jnp.transpose(chosen, (1, 2, 0))[:, :, None, :]
    strip = math.gcd(rows, 16)

    def one_strip(start):
        piece = lax.dynamic_slice_in_dim(padded, start, strip + 2 * half, 1)
        result = lax.conv_general_dilated(
            piece[None],
            filters,
            (1, 1),
            "VALID",
            dimension_numbers=("NCHW", "HWIO", "NCHW"),
            feature_group_count=count,
            precision=lax.Precision.HIGHEST,
        )
        return result[0]

    starts = jnp.arange(rows // strip, dtype=jnp.int32) * strip
    strips = lax.map(one_strip, starts)
    return jnp.transpose(strips, (1, 0, 2, 3)).reshape(count, rows, width)


def subtract(stack, reference_image, chosen, masks):
    result = reference_image[None] - correlate(stack, chosen)
    shape = result.shape
    tiles = result.reshape(shape[0], shape[1], shape[2] // 128, 128) * masks[..., None].astype(
        jnp.float32
    )
    return tiles.reshape(shape)


def build_design(systematics, onsets):
    count = systematics.shape[0]
    templates = onsets.shape[0]
    epoch_axis = jnp.arange(count, dtype=jnp.float32)[:, None]
    delays = epoch_axis - onsets[None, :].astype(jnp.float32)
    timescale = (jnp.arange(templates, dtype=jnp.float32) + 1.0) * count / (2.0 * templates)
    transient = jnp.where(
        delays >= 0.0, jnp.exp(-jnp.maximum(delays, 0.0) / timescale[None, :]), 0.0
    )
    return jnp.concatenate([systematics, transient], axis=1)


def fit_matrix(scatter, npixels, design):
    count = design.shape[0]
    columns = design.shape[1]
    covariance = scatter / npixels + cov_ridge * jnp.eye(count, dtype=scatter.dtype)
    lower = jnp.linalg.cholesky(covariance)
    weighted = jax.scipy.linalg.cho_solve((lower, True), design)
    normal = jnp.dot(design.T, weighted, precision=lax.Precision.HIGHEST) + fit_ridge * jnp.eye(
        columns, dtype=scatter.dtype
    )
    lower_fit = jnp.linalg.cholesky(normal)
    return jax.scipy.linalg.cho_solve((lower_fit, True), weighted.T)


def shards(images, reference_image, kernels, kernel_index, tile_mask, systematics, onsets):
    local_count, rows, width = images.shape
    basis = kernels.shape[0]
    side = kernels.shape[1]
    onehot = (kernel_index[:, None] == jnp.arange(basis, dtype=jnp.int32)[None, :]).astype(
        jnp.float32
    )
    chosen = jnp.dot(
        onehot, kernels.reshape(basis, side * side), precision=lax.Precision.HIGHEST
    ).reshape(local_count, side, side)
    difference = subtract(images, reference_image, chosen, tile_mask)
    received = lax.all_to_all(difference, "ep", split_axis=1, concat_axis=0, tiled=True)
    count = received.shape[0]
    block_rows = received.shape[1]
    pixel_data = received.reshape(count, block_rows * width)
    partial_value = jnp.dot(pixel_data, pixel_data.T, precision=lax.Precision.HIGHEST)
    scatter = lax.psum(partial_value, "ep")
    npixels = float(rows * width)
    design = build_design(systematics, onsets)
    fit = fit_matrix(scatter, npixels, design)
    coefficients = jnp.dot(fit, pixel_data, precision=lax.Precision.HIGHEST)
    projector = jnp.eye(count, dtype=jnp.float32) - jnp.dot(
        design, fit, precision=lax.Precision.HIGHEST
    )
    product = jnp.dot(projector, scatter, precision=lax.Precision.HIGHEST)
    epoch_scatter = jnp.sum(product * projector, axis=1) / npixels
    return (coefficients.reshape(design.shape[1], block_rows, width), epoch_scatter)


def solution(mesh):
    in_specs = (
        P(("field", "ep"), None, None),
        P("field", None),
        P(),
        P(("field", "ep")),
        P(("field", "ep"), None, None),
        P("field", None),
        P("field"),
    )
    out_specs = (P(None, ("field", "ep"), None), P("field"))
    return jax.shard_map(shards, mesh=mesh, in_specs=in_specs, out_specs=out_specs, check_vma=False)
```

profile of v0, /device:TPU:0, one launch (start us, length us, event | category | flops | bytes accessed | tf_op | source)
XLA Modules:
  0.0 186.9 jit_solution(5411633704186777744)
XLA Ops:
  0.6 0.8 pad_bitcast_fusion
  1.5 7.8 %copy.30 = f32[1,2,38,278]{1,0,3,2:T(1,128)} copy(f32[1,2,38,278]{3,2,1,0:T(8,128)S(1)} %pad_bitcast_fusion) | data formatting | bytes 169024 | tf_op jit(solution)/shard_map/while/body/eval_jaxpr/broadcast_in_dim | solution.py:22
  9.6 0.2 convolution_bitcast_fusion.1
  9.8 0.3 copy.31
  10.1 0.7 copy.32
  10.8 82.8 %fusion.21 = f32[1,2,16,256]{1,0,3,2:T(1,128)S(1)} fusion(f32[1,2,38,278]{1,0,3,2:T(1,128)} %copy.30, f32[23,23,1,2]{3,2,1,0:T(1,128)S(1)} %copy.31), kind=kOutput, calls=%fused_computation.46 | convolution fusion | flops 52002816 | bytes 121512 | tf_op jit(solution)/shard_map/while/body/eval_jaxpr/conv_general_dilated | solution.py:21
  93.6 0.9 bitcast_multiply_fusion
  94.5 1.2 copy.33
  95.8 7.4 %all-to-all-start = ((f32[2,16,256]{2,0,1:T(2,128)}), f32[2,16,256]{2,0,1:T(2,128)S(1)}, u32[]{:S(2)}, u32[]{:S(2)}) async-start(f32[2,16,256]{2,0,1:T(2,128)} %copy.33), calls=%async_computation | async-start | bytes 65536 | tf_op jit(solution)/shard_map/all_to_all | solution.py:82
  103.2 6.6 %all-to-all-done = f32[2,16,256]{2,0,1:T(2,128)S(1)} async-done(((f32[2,16,256]{2,0,1:T(2,128)}), f32[2,16,256]{2,0,1:T(2,128)S(1)}, u32[]{:S(2)}, u32[]{:S(2)}) %all-to-all-start) | async-done | bytes 32800 | tf_op jit(solution)/shard_map/all_to_all | solution.py:82
  110.0 57.7 %psum.7 = f32[32,32]{1,0:T(8,128)S(1)} all-reduce(f32[32,32]{1,0:T(8,128)S(1)} %fusion.22), channel_id=1, replica_groups=mesh['field'=2,'ep'=16] {'ep'}, use_global_device_ids=true, to_apply=%region_0.1 | all-reduce | flops 1024 | bytes 8192 | tf_op jit(solution)/shard_map/psum | solution.py:87
  167.8 2.9 %cholesky.34 = f32[32,32]{1,0:T(8,128)S(1)} custom-call(f32[32,32]{1,0:T(8,128)S(1)} %fusion.14), custom_call_target="Cholesky" | custom-call | tf_op jit(solution)/shard_map/jit(cholesky)/cholesky | solution.py:62
  170.7 0.6 compare_reduce_fusion.1
  171.4 0.7 fusion.9
  172.0 2.4 %custom-call.20 = f32[1,32,32]{1,2,0:T(8,128)S(1)} custom-call(f32[1,32,32]{2,1,0:T(8,128)S(1)} %fusion.9), custom_call_target="InvertDiagBlocksLowerTriangular" | custom-call | tf_op jit(solution)/shard_map/jit(_cho_solve)/triangular_solve | solution.py:63
  174.4 0.3 fusion.12
  174.8 0.3 fusion.20
  175.3 4.4 %cholesky.64 = f32[48,48]{1,0:T(8,128)S(1)} custom-call(f32[48,48]{1,0:T(8,128)S(1)} %fusion.8), custom_call_target="Cholesky" | custom-call | tf_op jit(solution)/shard_map/jit(cholesky)/cholesky | solution.py:67
  179.7 0.6 compare_reduce_fusion
  180.3 0.7 fusion.2
  181.0 3.7 %custom-call.21 = f32[1,48,48]{1,2,0:T(8,128)S(1)} custom-call(f32[1,48,48]{2,1,0:T(8,128)S(1)} %fusion.2), custom_call_target="InvertDiagBlocksLowerTriangular" | custom-call | tf_op jit(solution)/shard_map/jit(_cho_solve)/triangular_solve | solution.py:68
  185.5 0.2 fusion
  185.7 0.5 broadcast_multiply_fusion
  186.2 0.7 copy.38
  (35 shorter events, 1.7 us)
Async XLA Ops:
  1.5 7.8 %copy-start = (f32[16,23,23]{2,0,1:T(8,128)S(1)}, f32[16,23,23]{2,0,1:T(8,128)}, u32[]{:S(2)}) copy-start(f32[16,23,23]{2,0,1:T(8,128)} %param.9) | copy-start | bytes 101572
  1.5 8.1 %copy-start.5 = (s32[2]{0:T(128)S(1)}, s32[2]{0:T(128)}, u32[]{:S(2)}) copy-start(s32[2]{0:T(128)} %param.10) | copy-start | bytes 28
  1.5 8.6 %copy-start.4 = (s32[2,16,2]{1,2,0:T(2,128)S(1)}, s32[2,16,2]{1,2,0:T(2,128)}, u32[]{:S(2)}) copy-start(s32[2,16,2]{1,2,0:T(2,128)} %param.11) | copy-start | bytes 772
  10.8 82.8 %copy-start.2 = (f32[2,16,2]{0,2,1:T(2,128)S(1)}, f32[2,16,2]{0,2,1:T(2,128)}, u32[]{:S(2)}) copy-start(f32[2,16,2]{0,2,1:T(2,128)} %copy.32) | copy-start | bytes 772
  10.8 82.8 %copy-start.3 = (f32[16,256]{1,0:T(8,128)S(1)}, f32[16,256]{1,0:T(8,128)}, u32[]{:S(2)}) copy-start(f32[16,256]{1,0:T(8,128)} %param.8) | copy-start | bytes 49156
  94.5 8.7 %copy-start.6 = (s32[8]{0:T(128)S(1)}, s32[8]{0:T(128)}, u32[]{:S(2)}) copy-start(s32[8]{0:T(128)} %param.13) | copy-start | bytes 100
  94.5 79.9 %copy-start.1 = (f32[32,40]{1,0:T(8,128)S(1)}, f32[32,40]{1,0:T(8,128)}, u32[]{:S(2)}) copy-start(f32[32,40]{1,0:T(8,128)} %param.12) | copy-start | bytes 15364
  95.8 14.1 %all-to-all-start = ((f32[2,16,256]{2,0,1:T(2,128)}), f32[2,16,256]{2,0,1:T(2,128)S(1)}, u32[]{:S(2)}, u32[]{:S(2)}) async-start(f32[2,16,256]{2,0,1:T(2,128)} %copy.33), calls=%async_computation | async-start | bytes 65536 | tf_op jit(solution)/shard_map/all_to_all | solution.py:82
where the time goes:
time: 187 us
  matrix products  84.9 us (45%)
  blocking collectives  57.7 us (31%)
  other arithmetic  17.5 us (9%)
  local copies, waits for them, and re-layouts  12 us (6%)
  starting transfers between devices  7.41 us (4%)
  waiting for transfers between devices  6.57 us (4%)
    conv_general_dilated x1, matrix products, one_strip(): lax.conv_general_dilated(piece[None], filters, (1, 1), 'VALID', dimension...  82.8 us
    psum x1, blocking collectives, shards(): scatter = lax.psum(partial_value, 'ep')  57.7 us
    broadcast_in_dim x2, local copies, waits for them, and re-layouts, one_strip(): piece[None]  8.6 us
    all_to_all x1, starting transfers between devices, shards(): lax.all_to_all(difference, 'ep', split_axis=1, concat_axis=0, tiled=True)  7.41 us
    all_to_all x1, waiting for transfers between devices, shards(): lax.all_to_all(difference, 'ep', split_axis=1, concat_axis=0, tiled=True)  6.57 us
    another operation x3, other arithmetic, fit_matrix(): lower_fit = jnp.linalg.cholesky(normal)  5.05 us
    another operation x2, other arithmetic, fit_matrix(): return jax.scipy.linalg.cho_solve((lower_fit, True), weighted.T)  4.32 us
  transfers between devices with their start and end apart: 1, of which 1 were waited for; matrix products, arithmetic and copies ran while one was open for 0% of the time, Pallas kernels for 0%

commit v1 on v0

--- a/solution.py
+++ b/solution.py
@@ -84,7 +84,7 @@
     block_rows = received.shape[1]
     pixel_data = received.reshape(count, block_rows * width)
     partial_value = jnp.dot(pixel_data, pixel_data.T, precision=lax.Precision.HIGHEST)
-    scatter = lax.psum(partial_value, "ep")
+    scatter = jnp.sum(lax.all_gather(partial_value, "ep"), axis=0)
     npixels = float(rows * width)
     design = build_design(systematics, onsets)
     fit = fit_matrix(scatter, npixels, design)

time: 187 us -> 148 us (0.79)
  blocking collectives: 57.7 us -> 18.3 us
    psum x1 -> x0, blocking collectives: 57.7 us -> none  [shards(): scatter = lax.psum(partial_value, 'ep')]
    all_gather x0 -> x1, blocking collectives: none -> 18.3 us  [shards(): scatter = jnp.sum(lax.all_gather(partial_value, 'ep'), axis=0)]
where the time goes in v1:
time: 148 us
  matrix products  84.9 us (57%)
  blocking collectives  18.3 us (12%)
  other arithmetic  17.6 us (12%)
  local copies, waits for them, and re-layouts  12.1 us (8%)
  starting transfers between devices  7.41 us (5%)
  waiting for transfers between devices  6.57 us (4%)
    conv_general_dilated x1, matrix products, one_strip(): lax.conv_general_dilated(piece[None], filters, (1, 1), 'VALID', dimension...  82.8 us
    all_gather x1, blocking collectives, shards(): scatter = jnp.sum(lax.all_gather(partial_value, 'ep'), axis=0)  18.3 us
    broadcast_in_dim x2, local copies, waits for them, and re-layouts, one_strip(): piece[None]  8.6 us
    all_to_all x1, starting transfers between devices, shards(): lax.all_to_all(difference, 'ep', split_axis=1, concat_axis=0, tiled=True)  7.41 us
    all_to_all x1, waiting for transfers between devices, shards(): lax.all_to_all(difference, 'ep', split_axis=1, concat_axis=0, tiled=True)  6.57 us
    another operation x3, other arithmetic, fit_matrix(): lower_fit = jnp.linalg.cholesky(normal)  5.05 us
    another operation x2, other arithmetic, fit_matrix(): return jax.scipy.linalg.cho_solve((lower_fit, True), weighted.T)  4.32 us
    another operation x3, other arithmetic, fit_matrix(): lower = jnp.linalg.cholesky(covariance)  3.59 us
  transfers between devices with their start and end apart: 1, of which 1 were waited for; matrix products, arithmetic and copies ran while one was open for 0% of the time, Pallas kernels for 0%

profile of v1, /device:TPU:0, one launch (start us, length us, event | category | flops | bytes accessed | tf_op | source)
XLA Modules:
  0.0 147.6 jit_solution(16331697867244578750)
XLA Ops:
  0.6 0.8 pad_bitcast_fusion
  1.5 7.8 %copy.30 = f32[1,2,38,278]{1,0,3,2:T(1,128)} copy(f32[1,2,38,278]{3,2,1,0:T(8,128)S(1)} %pad_bitcast_fusion) | data formatting | bytes 169024 | tf_op jit(solution)/shard_map/while/body/eval_jaxpr/broadcast_in_dim | solution.py:22
  9.6 0.2 convolution_bitcast_fusion.1
  9.8 0.3 copy.31
  10.1 0.7 copy.32
  10.8 82.8 %fusion.22 = f32[1,2,16,256]{1,0,3,2:T(1,128)S(1)} fusion(f32[1,2,38,278]{1,0,3,2:T(1,128)} %copy.30, f32[23,23,1,2]{3,2,1,0:T(1,128)S(1)} %copy.31), kind=kOutput, calls=%fused_computation.48 | convolution fusion | flops 52002816 | bytes 121512 | tf_op jit(solution)/shard_map/while/body/eval_jaxpr/conv_general_dilated | solution.py:21
  93.6 0.9 bitcast_multiply_fusion
  94.5 1.2 copy.33
  95.8 7.4 %all-to-all-start = ((f32[2,16,256]{2,0,1:T(2,128)}), f32[2,16,256]{2,0,1:T(2,128)S(1)}, u32[]{:S(2)}, u32[]{:S(2)}) async-start(f32[2,16,256]{2,0,1:T(2,128)} %copy.33), calls=%async_computation | async-start | bytes 65536 | tf_op jit(solution)/shard_map/all_to_all | solution.py:82
  103.2 6.6 %all-to-all-done = f32[2,16,256]{2,0,1:T(2,128)S(1)} async-done(((f32[2,16,256]{2,0,1:T(2,128)}), f32[2,16,256]{2,0,1:T(2,128)S(1)}, u32[]{:S(2)}, u32[]{:S(2)}) %all-to-all-start) | async-done | bytes 32800 | tf_op jit(solution)/shard_map/all_to_all | solution.py:82
  110.0 18.3 %all-gather = f32[512,32]{1,0:T(8,128)S(1)} all-gather(f32[32,32]{1,0:T(8,128)S(1)} %fusion.23), channel_id=2, replica_groups=mesh['field'=2,'ep'=16] {'ep'}, dimensions={0}, use_global_device_ids=true | all-gather | bytes 69632 | tf_op jit(solution)/shard_map/all_gather | solution.py:87
  128.5 2.9 %cholesky.34 = f32[32,32]{1,0:T(8,128)S(1)} custom-call(f32[32,32]{1,0:T(8,128)S(1)} %fusion.15), custom_call_target="Cholesky" | custom-call | tf_op jit(solution)/shard_map/jit(cholesky)/cholesky | solution.py:62
  131.4 0.6 compare_reduce_fusion.1
  132.1 0.7 fusion.9
  132.7 2.4 %custom-call.20 = f32[1,32,32]{1,2,0:T(8,128)S(1)} custom-call(f32[1,32,32]{2,1,0:T(8,128)S(1)} %fusion.9), custom_call_target="InvertDiagBlocksLowerTriangular" | custom-call | tf_op jit(solution)/shard_map/jit(_cho_solve)/triangular_solve | solution.py:63
  135.2 0.3 fusion.12
  135.6 0.3 fusion.21
  136.0 4.4 %cholesky.64 = f32[48,48]{1,0:T(8,128)S(1)} custom-call(f32[48,48]{1,0:T(8,128)S(1)} %fusion.8), custom_call_target="Cholesky" | custom-call | tf_op jit(solution)/shard_map/jit(cholesky)/cholesky | solution.py:67
  140.4 0.6 compare_reduce_fusion
  141.0 0.7 fusion.2
  141.7 3.7 %custom-call.21 = f32[1,48,48]{1,2,0:T(8,128)S(1)} custom-call(f32[1,48,48]{2,1,0:T(8,128)S(1)} %fusion.2), custom_call_target="InvertDiagBlocksLowerTriangular" | custom-call | tf_op jit(solution)/shard_map/jit(_cho_solve)/triangular_solve | solution.py:68
  146.2 0.2 fusion
  146.4 0.5 broadcast_multiply_fusion.1
  146.9 0.7 copy.39
  (37 shorter events, 1.8 us)
Async XLA Ops:
  1.5 7.8 %copy-start = (f32[16,23,23]{2,0,1:T(8,128)S(1)}, f32[16,23,23]{2,0,1:T(8,128)}, u32[]{:S(2)}) copy-start(f32[16,23,23]{2,0,1:T(8,128)} %param.9) | copy-start | bytes 101572
  1.5 8.1 %copy-start.5 = (s32[2]{0:T(128)S(1)}, s32[2]{0:T(128)}, u32[]{:S(2)}) copy-start(s32[2]{0:T(128)} %param.10) | copy-start | bytes 28
  1.5 8.6 %copy-start.4 = (s32[2,16,2]{1,2,0:T(2,128)S(1)}, s32[2,16,2]{1,2,0:T(2,128)}, u32[]{:S(2)}) copy-start(s32[2,16,2]{1,2,0:T(2,128)} %param.11) | copy-start | bytes 772
  10.8 82.8 %copy-start.2 = (f32[2,16,2]{0,2,1:T(2,128)S(1)}, f32[2,16,2]{0,2,1:T(2,128)}, u32[]{:S(2)}) copy-start(f32[2,16,2]{0,2,1:T(2,128)} %copy.32) | copy-start | bytes 772
  10.8 82.8 %copy-start.3 = (f32[16,256]{1,0:T(8,128)S(1)}, f32[16,256]{1,0:T(8,128)}, u32[]{:S(2)}) copy-start(f32[16,256]{1,0:T(8,128)} %param.8) | copy-start | bytes 49156
  94.5 8.7 %copy-start.6 = (s32[8]{0:T(128)S(1)}, s32[8]{0:T(128)}, u32[]{:S(2)}) copy-start(s32[8]{0:T(128)} %param.13) | copy-start | bytes 100
  94.5 40.6 %copy-start.1 = (f32[32,40]{1,0:T(8,128)S(1)}, f32[32,40]{1,0:T(8,128)}, u32[]{:S(2)}) copy-start(f32[32,40]{1,0:T(8,128)} %param.12) | copy-start | bytes 15364
  95.8 14.1 %all-to-all-start = ((f32[2,16,256]{2,0,1:T(2,128)}), f32[2,16,256]{2,0,1:T(2,128)S(1)}, u32[]{:S(2)}, u32[]{:S(2)}) async-start(f32[2,16,256]{2,0,1:T(2,128)} %copy.33), calls=%async_computation | async-start | bytes 65536 | tf_op jit(solution)/shard_map/all_to_all | solution.py:82
